TPU v7x, 16 devices: a 4x2x1 block of a 4x4x8 slice. The times are simulated.
16 devices in a mesh: rep: 2 (over y, z), seq: 8 (over x, core).
Axes of the slice: x: 4, y: 2, z: 1, core: 2. Of those that a mesh axis runs over, the one named last changes fastest.
The devices are a block of a 4x4x8 slice.
Arguments:
- hidden: bfloat16 [128, 4096], P('rep'), parts along dimension 0
- w_query: bfloat16 [4096, 4096], replicated
- w_key: bfloat16 [4096, 1024], replicated
- w_value: bfloat16 [4096, 1024], replicated
- w_out: bfloat16 [4096, 4096], P('seq')
- k_cache: bfloat16 [128, 1024, 8, 128], P('rep', 'seq'), parts along dimension 0
- v_cache: bfloat16 [128, 1024, 8, 128], P('rep', 'seq'), parts along dimension 0
- positions: int32 [128], P('rep'), parts along dimension 0
Outputs:
- output 1: bfloat16 [128, 4096], P('rep'), parts along dimension 0
- output 2: bfloat16 [128, 1024, 8, 128], P('rep', 'seq'), parts along dimension 0
- output 3: bfloat16 [128, 1024, 8, 128], P('rep', 'seq'), parts along dimension 0
There are 2 independent parts. A program takes and returns all parts, laid end to end along the dimension named above; an argument that names none is the same for every part.
All inputs are finite; a program needn't handle non-finite values.
Results may differ from a plain program's by a relative error of at most 0.00593277.
Values are sent between devices in bfloat16 or wider.
A program may use at most 768 MiB of HBM per device.

v0:
```python
import jax
import jax.numpy as jnp
from jax import lax
from jax.sharding import PartitionSpec as P


def solution(mesh):
    cache_spec = P('rep', 'seq', None, None)
    in_specs = (P('rep', None), P(), P(), P(), P('seq', None), cache_spec, cache_spec, P('rep'))
    out_specs = (P('rep', None), cache_spec, cache_spec)

    def local_step(hidden, w_query, w_key, w_value, w_out, k_cache, v_cache, positions):
        batch_size, local_len, kv_heads, head_dim = k_cache.shape
        num_heads = w_query.shape[1] // head_dim
        group_size = num_heads // kv_heads
        shard_idx = lax.axis_index('seq')
        q_flat = jnp.dot(hidden, w_query, preferred_element_type=jnp.float32).astype(jnp.bfloat16)
        key_new = jnp.dot(hidden, w_key, preferred_element_type=jnp.float32).astype(jnp.bfloat16).reshape(batch_size, kv_heads, head_dim)
        value_new = jnp.dot(hidden, w_value, preferred_element_type=jnp.float32).astype(jnp.bfloat16).reshape(batch_size, kv_heads, head_dim)
        seq_ids = shard_idx * local_len + jnp.arange(local_len)
        at_pos = (seq_ids[None, :] == positions[:, None])[:, :, None, None]
        k_updated = jnp.where(at_pos, key_new[:, None], k_cache)
        v_updated = jnp.where(at_pos, value_new[:, None], v_cache)
        is_valid = (seq_ids[None, :] <= positions[:, None])[:, None, None, :]
        q_heads = q_flat.reshape(batch_size, kv_heads, group_size, head_dim)
        scores = jnp.einsum('bkgd,bskd->bkgs', q_heads, k_updated, preferred_element_type=jnp.float32) * head_dim ** -0.5
        scores = jnp.where(is_valid, scores, -jnp.inf)
        local_max = jnp.max(scores, axis=-1)
        safe_max = jnp.where(jnp.isfinite(local_max), local_max, 0.0)
        weights = jnp.exp(scores - safe_max[..., None])
        local_sum = jnp.sum(weights, axis=-1)
        local_out = jnp.einsum('bkgs,bskd->bkgd', weights.astype(jnp.bfloat16), v_updated, preferred_element_type=jnp.float32)
        global_max = lax.pmax(local_max, 'seq')
        rescale = jnp.exp(local_max - global_max)
        total_sum, total_out = lax.psum((local_sum * rescale, local_out * rescale[..., None]), 'seq')
        combined = (total_out / total_sum[..., None]).astype(jnp.bfloat16).reshape(batch_size, num_heads * head_dim)
        row_count = w_out.shape[0]
        combined_rows = lax.dynamic_slice_in_dim(combined, shard_idx * row_count, row_count, axis=1)
        part_out = jnp.dot(combined_rows, w_out, preferred_element_type=jnp.float32)
        result = lax.psum(part_out, 'seq').astype(jnp.bfloat16)
        return result, k_updated, v_updated

    return jax.shard_map(local_step, mesh=mesh, in_specs=in_specs, out_specs=out_specs, check_vma=False)
```

profile of v0, /device:TPU:113, one launch (start us, length us, event | category | flops | bytes accessed | tf_op | source)
XLA Modules:
  0.0 225.6 jit_solution(18391956327885880515)
XLA Ops:
  7.2 0.0 copy-start
  7.2 0.1 all-reduce.3.cloned.1.call-start
  7.3 0.0 slice-start
  7.3 0.9 copy-done
  8.2 0.0 slice-start.1
  8.2 5.3 %fusion.10 = bf16[8,8,8,128]{3,1,2,0:T(8,128)(2,1)S(1)} fusion(bf16[64,4096]{1,0:T(8,128)(2,1)S(1)} %copy-done, bf16[4096,1024]{1,0:T(8,128)(2,1)} %param.10), kind=kOutput, calls=%fused_computation.11 | convolution fusion | flops 536936448 | bytes 9043968 | tf_op jit(solution)/shard_map/dot_general | solution.py:18
  13.6 0.0 slice-done
  13.6 0.0 slice-done.1
  13.6 1.6 fusion.11
  15.3 0.0 copy-start.3
  15.3 13.6 %convolution_convert_fusion = bf16[64,4096]{1,0:T(8,128)(2,1)S(1)} fusion(bf16[64,4096]{1,0:T(8,128)(2,1)S(1)} %copy-done, bf16[4096,4096]{1,0:T(8,128)(2,1)} %param.9), kind=kOutput, calls=%fused_computation.6 | convolution fusion | flops 2147745792 | bytes 34603008 | tf_op jit(solution)/shard_map/dot_general | solution.py:17
  28.9 1.2 reshape.73
  30.1 0.0 copy-done.3
  30.1 0.1 broadcast_compare_fusion.1
  30.2 17.4 %broadcast_select_fusion.1 = (bf16[64,128,8,128]{3,2,1,0:T(8,128)(2,1)S(1)}, bf16[64,128,8,128]{3,2,1,0:T(8,128)(2,1)}) fusion(bf16[64,128,8,128]{3,2,1,0:T(8,128)(2,1)} %param.13, pred[64,128]{1,0:T(8,128)(4,1)S(1)} %get-tuple-element.8, bf16[64,8,128]{2,1,0:T(8,128)(2,1)S(1)} %bitcast.16, bf16[64,128,8,128]{3,2,1,0:T(8,128)(2,1)} %param.14, ...), kind=kLoop, calls=%fused_computation.5 | loop fusion | flops 16777216 | bytes 67379200 | tf_op jit(solution)/shard_map/jit(_where)/select_n | solution.py:22
  47.5 0.0 copy-start.2
  47.5 6.2 %copy-done.2 = bf16[64,128,8,128]{3,2,1,0:T(8,128)(2,1)} copy-done((bf16[64,128,8,128]{3,2,1,0:T(8,128)(2,1)}, bf16[64,128,8,128]{3,2,1,0:T(8,128)(2,1)S(1)}, u32[]{:S(2)}) %copy-start.2) | copy-done | bytes 16777240
  53.7 10.9 %fusion.23 = (f32[64,8,4]{2,1,0:T(8,128)S(1)}, f32[64,8,4,128]{3,2,1,0:T(4,128)}) fusion(bf16[64,8,4,128]{3,2,1,0:T(4,128)(2,1)} %reshape.73, bf16[64,128,8,128]{3,2,1,0:T(8,128)(2,1)S(1)} %get-tuple-element.5, pred[64,128]{1,0:T(8,128)(4,1)S(1)} %get-tuple-element.7), kind=kOutput, calls=%fused_computation.28 | convolution fusion | flops 67893248 | bytes 18366464 | tf_op jit(solution)/shard_map/bkgd,bskd->bkgs/dot_general | solution.py:26
  64.6 26.9 %pmax.7 = f32[64,8,4]{2,1,0:T(8,128)S(1)} all-reduce(f32[64,8,4]{2,1,0:T(8,128)S(1)} %get-tuple-element.9), channel_id=1, replica_groups=mesh['rep'=2,'seq'=8] {'seq'}, use_global_device_ids=true, to_apply=%region_1.2 | all-reduce | flops 2048 | bytes 16384 | tf_op jit(solution)/shard_map/pmax | solution.py:33
  91.5 2.4 %fusion.15 = f32[64,8,4]{2,1,0:T(8,128)S(1)} fusion(f32[64,8,4,128]{3,2,1,0:T(4,128)} %get-tuple-element.10, f32[64,8,4]{2,1,0:T(8,128)S(1)} %is-finite_select_fusion), kind=kLoop, calls=%fused_computation.16 | loop fusion | flops 522240 | bytes 1064960 | tf_op jit(solution)/shard_map/reduce_sum | solution.py:31
  93.9 0.1 fusion.22
  93.9 0.0 copy-start.1
  94.0 11.5 %fusion.7 = f32[64,8,4,128]{3,2,1,0:T(4,128)} fusion(bf16[64,128,8,128]{3,2,1,0:T(8,128)(2,1)} %get-tuple-element.6, f32[64,8,4,128]{3,2,1,0:T(4,128)} %get-tuple-element.10, f32[64,8,4]{2,1,0:T(8,128)S(1)} %get-tuple-element.4, f32[64,8,4]{2,1,0:T(8,128)S(1)} %is-finite_select_fusion), kind=kOutput, calls=%fused_computation.8 | convolution fusion | flops 67895296 | bytes 18890752 | tf_op jit(solution)/shard_map/bkgs,bskd->bkgd/dot_general | solution.py:32
  105.5 0.1 all-reduce.3.cloned.1.call-update
  105.5 27.1 %psum.22 = f32[64,8,4]{2,1,0:T(8,128)S(1)} all-reduce(f32[64,8,4]{2,1,0:T(8,128)S(1)} %get-tuple-element.3), channel_id=1, replica_groups=mesh['rep'=2,'seq'=8] {'seq'}, use_global_device_ids=true, to_apply=%region_4.5 | all-reduce | flops 2048 | bytes 16384 | tf_op jit(solution)/shard_map/psum | solution.py:35
  132.6 28.6 %all-reduce.3.cloned.1.call-done = f32[64,8,4,128]{3,2,1,0:T(4,128)} async-done(((f32[64,8,4,128]{3,2,1,0:T(4,128)}), f32[64,8,4,128]{3,2,1,0:T(4,128)}) %all-reduce.3.cloned.1.call-update) | async-done | bytes 1048592 | tf_op jit(solution)/shard_map/psum | solution.py:35
  161.2 1.8 divide_convert_fusion
  163.0 0.4 reshape.74
  163.3 3.0 %fusion.19 = f32[64,4096]{1,0:T(8,128)S(1)} fusion(bf16[512,4096]{1,0:T(8,128)(2,1)} %param.12, bf16[64,4096]{1,0:T(8,128)(2,1)S(1)} %reshape.74, s32[]{:T(128)S(6)} %select_n.26), kind=kOutput, calls=%fused_computation.21 | convolution fusion | flops 268435456 | bytes 5308420 | tf_op jit(solution)/shard_map/dot_general | solution.py:39
  166.4 52.4 %all-reduce.4 = bf16[64,4096]{1,0:T(8,128)(2,1)} all-reduce(f32[64,4096]{1,0:T(8,128)S(1)} %fusion.19), channel_id=1, replica_groups=mesh['rep'=2,'seq'=8] {'seq'}, use_global_device_ids=true, to_apply=%region_5.6 | all-reduce | flops 262144 | bytes 1572864 | tf_op jit(solution)/shard_map/psum | solution.py:40
  218.8 0.0 copy-done.1
  (5 shorter events, 0.1 us)
Async XLA Ops:
  7.2 1.1 copy-start
  7.2 154.0 %all-reduce.3.cloned.1.call-start = ((), (), s32[]{:S(2)}) async-start(), calls=%async_computation | async-start | bytes 2097152 | tf_op jit(solution)/shard_map/psum | solution.py:35
  7.3 6.3 %slice-start = ((s8[8388608]{0:T(1024)(128)(4,1)}), s8[4194304]{0:T(1024)(128)(4,1)S(1)}, s32[]{:S(2)}) async-start(s8[8388608]{0:T(1024)(128)(4,1)} %bitcast.14), calls=%async_computation.1 | async-start | bytes 8388608
  8.2 5.4 %slice-start.1 = ((s8[8388608]{0:T(1024)(128)(4,1)}), s8[4194304]{0:T(1024)(128)(4,1)S(1)}, s32[]{:S(2)}) async-start(s8[8388608]{0:T(1024)(128)(4,1)} %bitcast.14), calls=%async_computation.2 | async-start | bytes 8388608
  15.3 14.8 %copy-start.3 = (s32[64]{0:T(128)S(1)}, s32[64]{0:T(128)}, u32[]{:S(2)}) copy-start(s32[64]{0:T(128)} %param.15) | copy-start | bytes 772
  47.5 6.2 %copy-start.2 = (bf16[64,128,8,128]{3,2,1,0:T(8,128)(2,1)}, bf16[64,128,8,128]{3,2,1,0:T(8,128)(2,1)S(1)}, u32[]{:S(2)}) copy-start(bf16[64,128,8,128]{3,2,1,0:T(8,128)(2,1)S(1)} %get-tuple-element.5) | copy-start | bytes 50331652
  93.9 124.8 %copy-start.1 = (bf16[64,4096]{1,0:T(8,128)(2,1)S(1)}, bf16[64,4096]{1,0:T(8,128)(2,1)}, u32[]{:S(2)}) copy-start(bf16[64,4096]{1,0:T(8,128)(2,1)} %param.8) | copy-start | bytes 1572868
Sparse Core Ops, SparseCore 0:
  105.7 55.4 all-reduce.2
where the time goes:
time: 227 us; the launch traced here: 226 us
  blocking collectives  106 us (47%)
  matrix products  46 us (20%)
  waiting for transfers between devices  28.6 us (13%)
  other arithmetic  21.6 us (10%)
  between operations  14.2 us (6%)
  local copies, waits for them, and re-layouts  8.72 us (4%)
    psum x1, blocking collectives, local_step(): result = lax.psum(part_out, 'seq').astype(jnp.bfloat16)  52.4 us
    psum x1, waiting for transfers between devices, local_step(): lax.psum((local_sum * rescale, local_out * rescale[..., None]), 'seq')  28.6 us
    psum x1, blocking collectives, local_step(): lax.psum((local_sum * rescale, local_out * rescale[..., None]), 'seq')  27.1 us
    pmax x1, blocking collectives, local_step(): global_max = lax.pmax(local_max, 'seq')  26.9 us
    select_n x1, other arithmetic, local_step(): k_updated = jnp.where(at_pos, key_new[:, None], k_cache)  17.4 us
    dot_general x1, matrix products, local_step(): jnp.dot(hidden, w_query, preferred_element_type=jnp.float32)  13.6 us
    dot_general x1, matrix products, local_step(): jnp.einsum('bkgs,bskd->bkgd', weights.astype(jnp.bfloat16), v_updated, pr...  11.5 us
    dot_general x1, matrix products, local_step(): jnp.einsum('bkgd,bskd->bkgs', q_heads, k_updated, preferred_element_type=...  10.9 us
  transfers between devices with their start and end apart: 1, of which 1 were waited for; matrix products, arithmetic and copies ran while one was open for 0% of the time, Pallas kernels for 0%

commit v1 on v0

v1 whole, which is shorter than its diff:
```python
import functools
import math

import jax
import jax.numpy as jnp
from jax import lax
from jax.experimental import pallas as pl
from jax.experimental.pallas import tpu as pltpu
from jax.sharding import PartitionSpec as P

MESH = pl.DeviceIdType.MESH
NEG = -3.4028234e38
F32, BF16 = jnp.float32, jnp.bfloat16
CORES = 2
NT = (((1,), (1,)), ((), ()))


def step_kernel(chips, x_hbm, wq_hbm, wk_hbm, wv_hbm, wo_hbm, k_hbm, v_hbm, pos_ref, pos2_ref,
                y_ref, kout, vout, kv_all,
                x_v, wbuf, wo_v, qs, q_all, colmask, oraw, mraw, lraw, om, op, orecv, ofin,
                ys, yp, yr, yfull,
                lsem, kvsem, q_ss, q_rs, n_ss, n_rs, od_s, od_r, oi_s, oi_r, yd_s, yd_r, yi_s, yi_r, ag_s, ag_r):
    batch = k_hbm.shape[0]
    local_len = k_hbm.shape[1] // 8
    chunks = om.shape[0]
    cb = batch // chunks
    half = batch // 2
    scale2 = k_hbm.shape[2] ** -0.5 * math.log2(math.e)
    rep = lax.axis_index('rep')
    me = lax.axis_index('seq')
    chip, core = me // CORES, me % CORES
    base = me * local_len
    quarter = (chip % 2) * CORES + core

    def dev(c, e):
        return (rep, lax.rem(c, chips) * CORES + e)

    partner = dev(chip, 1 - core)

    ncols = 256
    lx = pltpu.make_async_copy(x_hbm, x_v, lsem.at[0])
    lw = [pltpu.make_async_copy(wq_hbm.at[:, pl.ds(pl.multiple_of(quarter * 1024 + i * 512, 512), 512)], wbuf.at[i], lsem.at[1 + i])
          for i in range(2)]
    lk = pltpu.make_async_copy(wk_hbm.at[:, pl.ds(pl.multiple_of(quarter * ncols, ncols), ncols)], wbuf.at[2, :, pl.ds(0, ncols)], lsem.at[3])
    lv = pltpu.make_async_copy(wv_hbm.at[:, pl.ds(pl.multiple_of(quarter * ncols, ncols), ncols)], wbuf.at[2, :, pl.ds(ncols, ncols)], lsem.at[4])
    lo = pltpu.make_async_copy(wo_hbm, wo_v, lsem.at[5])
    lkc = [pltpu.make_async_copy(k_hbm.at[pl.ds(i * cb, cb)], kout.at[pl.ds(i * cb, cb)], kvsem.at[0, i]) for i in range(chunks)]
    lvc = [pltpu.make_async_copy(v_hbm.at[pl.ds(i * cb, cb)], vout.at[pl.ds(i * cb, cb)], kvsem.at[1, i]) for i in range(chunks)]
    lx.start()
    lw[0].start()
    lw[1].start()

    barrier = pltpu.get_barrier_semaphore()
    for d in range(chips):
        for f in range(CORES):
            if d or f:
                pl.semaphore_signal(barrier, inc=1, device_id=dev(chip + d, lax.rem(core + f, CORES)), device_id_type=MESH)

    row = lax.broadcasted_iota(jnp.int32, colmask.shape, 0)
    col = lax.broadcasted_iota(jnp.int32, colmask.shape, 1)
    colmask[...] = jnp.where(col % 8 == (row // 16) * 2 + (row % 8) // 4, col, 1 << 30)

    lx.wait()
    lk.start()
    lv.start()
    for i in range(2):
        lw[i].wait()
        if i == 0:
            lkc[0].start()
            lvc[0].start()
        q = jnp.dot(x_v[...], wbuf[i], preferred_element_type=F32)
        for h in range(4):
            qs[pl.ds(i * 4 + h, batch, stride=8), :] = q[:, h * 128:(h + 1) * 128]
    q_all[quarter] = qs[...].astype(BF16)
    pl.semaphore_wait(barrier, chips * CORES - 1)

    def spread(buf, rows, ss, rs):
        copies = [pltpu.make_async_remote_copy(buf.at[quarter], buf.at[quarter], ss.at[0], rs.at[0], device_id=partner, device_id_type=MESH)]
        for side, shift in ((0, 1), (1, chips - 1)):
            part = pl.ds(side * rows // 2, rows // 2)
            for f in range(CORES):
                e = lax.rem(core + f, CORES)
                slot = 1 + side * 2 + f
                copies.append(pltpu.make_async_remote_copy(
                    buf.at[quarter, part], buf.at[quarter, part], ss.at[slot], rs.at[slot], device_id=dev(chip + shift, e), device_id_type=MESH))
        return copies

    q_copies = spread(q_all, batch * 8, q_ss, q_rs)
    for c in q_copies:
        c.start()
    lk.wait()
    lv.wait()
    lkc[1].start()
    lvc[1].start()
    kv = jnp.dot(x_v[...], wbuf[2], preferred_element_type=F32)
    for w in range(2):
        for k in range(2):
            qs[pl.ds(w * 128 + k, batch, stride=2), :] = kv[:, w * 256 + k * 128:w * 256 + (k + 1) * 128]
    for hf in range(2):
        for w in range(2):
            kv_all[quarter, hf * 128 + w * 64:hf * 128 + w * 64 + 64, :] = qs[w * 128 + hf * 64:w * 128 + hf * 64 + 64, :].astype(BF16)
    n_copies = spread(kv_all, batch * 4, n_ss, n_rs)
    for c in n_copies:
        c.start()
    for i in range(2, chunks):
        lkc[i].start()
        lvc[i].start()
    lo.start()

    rowb = lax.broadcasted_iota(jnp.int32, (64, 128), 0) // 8 % 2
    bm0 = jnp.where(rowb == 0, 1.0, 0.0).astype(BF16)
    bm1 = jnp.where(rowb == 1, 1.0, 0.0).astype(BF16)

    for c in q_copies:
        c.wait_recv()

    def pair(pi, loc):
        q = jnp.concatenate([q_all[t, pl.ds(pl.multiple_of(pi * 16, 16), 16), :] for t in range(4)], axis=0)
        lhs = jnp.concatenate([q * bm0, q * bm1], axis=1)
        kcat = jnp.concatenate([kout[2 * pi], kout[2 * pi + 1]], axis=1)
        s = lax.dot_general(lhs, kcat, NT, preferred_element_type=F32)
        lim0 = (pos_ref[2 * pi] - base) * 8
        lim1 = (pos_ref[2 * pi + 1] - base) * 8
        lim = jnp.where(lax.broadcasted_iota(jnp.int32, (16, 1), 0) < 8, lim0, lim1)
        ps = []
        for t in range(4):
            st = jnp.where(colmask[t * 16:(t + 1) * 16, :] < lim, s[t * 16:(t + 1) * 16, :], -jnp.inf)
            m = jnp.maximum(jnp.max(st, axis=1, keepdims=True), NEG)
            p = jnp.exp2((st - m) * scale2)
            mraw[t, pl.ds(pl.multiple_of(loc * 16, 16), 16), :] = jnp.broadcast_to(m, (16, 128))
            lraw[t, pl.ds(pl.multiple_of(loc * 16, 16), 16), :] = jnp.broadcast_to(jnp.sum(p, axis=1, keepdims=True), (16, 128))
            ps.append(p.astype(BF16))
        vcat = jnp.concatenate([vout[2 * pi], vout[2 * pi + 1]], axis=1)
        o = jnp.dot(jnp.concatenate(ps, axis=0), vcat, preferred_element_type=F32)
        for t in range(4):
            for b in range(2):
                r = t * 16 + b * 8
                oraw[t, pl.ds(pl.multiple_of(loc * 16 + b * 8, 8), 8), :] = o[r:r + 8, b * 128:(b + 1) * 128]

    rows_c = cb * 8
    ppc = cb // 2

    def attend(i, sub):
        def body(j, carry):
            loc = sub * (ppc // 2) + j * 2
            pair(i * ppc + loc, loc)
            pair(i * ppc + loc + 1, loc + 1)
            return carry
        lax.fori_loop(0, ppc // 4, body, 0)

    lane = lax.broadcasted_iota(jnp.int32, (8, 128), 1)
    od, oi, yd, yi, ag = {}, {}, {}, {}, {}

    def finalize(i):
        hf = i * cb // half
        first = i * rows_c - hf * half * 8
        rr = lax.broadcasted_iota(jnp.int32, (rows_c, 64), 0) + first
        cc = lax.broadcasted_iota(jnp.int32, (rows_c, 64), 1)
        rel = pos2_ref[hf:hf + 1, :] - base
        keep = (rr // 4 == cc) & (rel >= 0) & (rel < local_len)
        for t in range(4):
            qt = q_all[t, i * rows_c:(i + 1) * rows_c, :]
            sn = lax.dot_general(qt, kv_all[t, hf * 128:hf * 128 + 64, :], NT, preferred_element_type=F32)
            sn = jnp.where(keep, sn, -jnp.inf)
            mo = mraw[t]
            mn = jnp.maximum(mo, jnp.max(sn, axis=1, keepdims=True))
            pn = jnp.exp2((sn - mn[:, :64]) * scale2)
            w = jnp.exp2((mo - mn) * scale2)
            lraw[t] = lraw[t] * w + jnp.sum(pn, axis=1, keepdims=True)
            oraw[t] = oraw[t] * w + jnp.dot(pn.astype(BF16), kv_all[t, hf * 128 + 64:hf * 128 + 128, :], preferred_element_type=F32)
            mraw[t] = mn
        for e in range(CORES):
            for t in range(4):
                mt = jnp.zeros((8, 128), F32)
                lt = jnp.zeros((8, 128), F32)
                for h in range(4):
                    src = pl.ds(e * 4 + h, cb, stride=8)
                    om[i, e, t, h * cb:(h + 1) * cb, :] = oraw[t, src, :]
                    mh = mraw[t, src, :]
                    lh = lraw[t, src, :]
                    for g in range(cb // 8):
                        sel = lane == h * (cb // 8) + g
                        mt = jnp.where(sel, mh[g * 8:(g + 1) * 8], mt)
                        lt = jnp.where(sel, lh[g * 8:(g + 1) * 8], lt)
                om[i, e, t, cb * 4:cb * 4 + 8, :] = mt
                om[i, e, t, cb * 4 + 8:cb * 4 + 16, :] = lt
        od[i] = pltpu.make_async_remote_copy(om.at[i, 1 - core], op.at[i], od_s.at[i], od_r.at[i], device_id=partner, device_id_type=MESH)
        od[i].start()

    nrow = cb * 4

    def merge(parts):
        ms = [p[nrow:nrow + 8] for p in parts]
        m = functools.reduce(jnp.maximum, ms)
        ws = [jnp.exp2((x - m) * scale2) for x in ms]
        l = functools.reduce(jnp.add, [w * p[nrow + 8:nrow + 16] for w, p in zip(ws, parts)])
        return m, l, ws

    def chip_reduce(i):
        od[i].wait_recv()
        for t in range(4):
            a, b = om[i, core, t], op[i, t]
            m, l, (wa, wb) = merge([a, b])
            for g in range(nrow // 8):
                r = slice(g * 8, g * 8 + 8)
                om[i, core, t, g * 8:g * 8 + 8, :] = a[r] * wa[:, g:g + 1] + b[r] * wb[:, g:g + 1]
            om[i, core, t, nrow:nrow + 8, :] = m
            om[i, core, t, nrow + 8:nrow + 16, :] = l
        oi[i] = []
        for d in range(1, chips):
            c = pltpu.make_async_remote_copy(om.at[i, core, lax.rem(chip + d, chips)], orecv.at[i, d - 1], oi_s.at[i, d - 1], oi_r.at[i, d - 1],
                                             device_id=dev(chip + d, core), device_id_type=MESH)
            c.start()
            oi[i].append(c)

    def project(i):
        for c in oi[i]:
            c.wait_recv()
        if i == 0:
            lo.wait()
        parts = [om[i, core, chip]] + [orecv[i, d] for d in range(chips - 1)]
        m, l, ws = merge(parts)
        rl = 1.0 / l
        heads = []
        for h in range(4):
            rows = []
            for g in range(h * (cb // 8), (h + 1) * (cb // 8)):
                o = functools.reduce(jnp.add, [p[g * 8:g * 8 + 8] * w[:, g:g + 1] for p, w in zip(parts, ws)])
                rows.append(o * rl[:, g:g + 1])
            heads.append(jnp.concatenate(rows, axis=0).astype(BF16))
        lhs = jnp.concatenate(heads, axis=1)
        for e in range(CORES):
            for t in range(4):
                c0 = (e * 4 + t) * 512
                ys[i, e, t] = jnp.dot(lhs, wo_v[:, c0:c0 + 512], preferred_element_type=F32)
        yd[i] = pltpu.make_async_remote_copy(ys.at[i, 1 - core], yp.at[i], yd_s.at[i], yd_r.at[i], device_id=partner, device_id_type=MESH)
        yd[i].start()

    def y_chip(i):
        yd[i].wait_recv()
        ys[i, core] = ys[i, core] + yp[i]
        yi[i] = []
        for d in range(1, chips):
            c = pltpu.make_async_remote_copy(ys.at[i, core, lax.rem(chip + d, chips)], yr.at[i, d - 1], yi_s.at[i, d - 1], yi_r.at[i, d - 1],
                                             device_id=dev(chip + d, core), device_id_type=MESH)
            c.start()
            yi[i].append(c)

    def y_final(i):
        for c in yi[i]:
            c.wait_recv()
        y = ys[i, core, chip]
        for d in range(chips - 1):
            y = y + yr[i, d]
        own = (pl.ds(i * cb, cb), pl.ds(pl.multiple_of((core * 4 + chip) * 512, 512), 512))
        yfull[own] = y.astype(BF16)
        ag[i] = []
        for d in range(chips):
            for f in range(CORES):
                if d or f:
                    slot = d * CORES + f - 1
                    c = pltpu.make_async_remote_copy(yfull.at[own], yfull.at[own], ag_s.at[i, slot], ag_r.at[i, slot],
                                                     device_id=dev(chip + d, lax.rem(core + f, CORES)), device_id_type=MESH)
                    c.start()
                    ag[i].append(c)

    stages = ((finalize, 1), (chip_reduce, 2), (project, 4), (y_chip, 5), (y_final, 7))
    for k in range(2 * chunks + 6):
        if k < 2 * chunks:
            if k % 2 == 0:
                lkc[k // 2].wait()
                lvc[k // 2].wait()
            attend(k // 2, k % 2)
        if k == 1:
            for c in n_copies:
                c.wait_recv()
        for stage, lag in stages:
            i = (k - lag) // 2
            if (k - lag) % 2 == 0 and 0 <= i < chunks:
                stage(i)
    for i in range(chunks):
        for c in ag[i]:
            c.wait_recv()
    y_ref[...] = yfull[...]
    for c in q_copies + n_copies:
        c.wait_send()
    for i in range(chunks):
        for c in [od[i], yd[i]] + oi[i] + yi[i] + ag[i]:
            c.wait_send()


def patch_kernel(k_in, v_in, new_ref, pos_ref, k_ref, v_ref, src, dst):
    batch = k_ref.shape[0]
    local_len = k_ref.shape[1]
    base = lax.axis_index('seq') * local_len
    hb = batch // 2
    for t in range(4):
        src[t] = new_ref[t].astype(F32)
    for w in range(2):
        for t in range(4):
            for hf in range(2):
                for k in range(2):
                    dst[w, pl.ds(hf * hb * 8 + t * 2 + k, hb, stride=8), :] = src[t, pl.ds(hf * 128 + w * 64 + k, hb, stride=2), :]

    def body(b, carry):
        rel = pos_ref[b] - base

        @pl.when((rel >= 0) & (rel < local_len))
        def _():
            r = pl.ds(pl.multiple_of(b * 8, 8), 8)
            k_ref[b, rel] = dst[0, r, :].astype(BF16)
            v_ref[b, rel] = dst[1, r, :].astype(BF16)
        return carry
    lax.fori_loop(0, batch, body, 0)


def solution(mesh):
    cache_spec = P('rep', 'seq', None, None)
    in_specs = (P('rep', None), P(), P(), P(), P('seq', None), cache_spec, cache_spec, P('rep'))
    out_specs = (P('rep', None), cache_spec, cache_spec)
    chips = mesh.shape['seq'] // CORES
    vm = pl.BlockSpec(memory_space=pltpu.VMEM)
    hbm = pl.BlockSpec(memory_space=pl.ANY)
    sm = pl.BlockSpec(memory_space=pltpu.SMEM)

    def local_step(x, wq, wk, wv, wo, k, v, pos):
        shape4 = k.shape
        batch, width = x.shape
        k3 = k.reshape(batch, -1, k.shape[-1])
        v3 = v.reshape(k3.shape)
        chunks = 4
        cb = batch // chunks
        dma = pltpu.SemaphoreType.DMA
        in_hbm = lambda a: pltpu.with_memory_space_constraint(a, pltpu.HBM)
        in_vmem = lambda a: pltpu.with_memory_space_constraint(a, pltpu.VMEM)
        pos2 = jnp.repeat(pos, 2).reshape(2, batch)
        y, ko, vo, new = pl.pallas_call(
            functools.partial(step_kernel, chips),
            out_shape=(jax.ShapeDtypeStruct((batch, wo.shape[1]), BF16), pltpu.VMEM(k3.shape, BF16), pltpu.VMEM(k3.shape, BF16),
                       jax.ShapeDtypeStruct((4, batch * 4, 128), BF16)),
            in_specs=[hbm] * 7 + [sm, vm],
            out_specs=[vm] * 4,
            scratch_shapes=[
                pltpu.VMEM((batch, width), BF16), pltpu.VMEM((3, width, 512), BF16), pltpu.VMEM(wo.shape, BF16),
                pltpu.VMEM((batch * 8, 128), F32), pltpu.VMEM((4, batch * 8, 128), BF16), pltpu.VMEM((64, k3.shape[1]), jnp.int32),
                pltpu.VMEM((4, cb * 8, 128), F32), pltpu.VMEM((4, cb * 8, 128), F32), pltpu.VMEM((4, cb * 8, 128), F32),
                pltpu.VMEM((chunks, CORES, 4, cb * 4 + 16, 128), F32), pltpu.VMEM((chunks, 4, cb * 4 + 16, 128), F32),
                pltpu.VMEM((chunks, chips - 1, cb * 4 + 16, 128), F32), pltpu.VMEM((cb * 4, 128), F32),
                pltpu.VMEM((chunks, CORES, 4, cb, 512), F32), pltpu.VMEM((chunks, 4, cb, 512), F32), pltpu.VMEM((chunks, chips - 1, cb, 512), F32),
                pltpu.VMEM((batch, wo.shape[1]), BF16),
                dma((6,)), dma((2, chunks)), dma((5,)), dma((5,)), dma((5,)), dma((5,)), dma((chunks,)), dma((chunks,)),
                dma((chunks, chips - 1)), dma((chunks, chips - 1)), dma((chunks,)), dma((chunks,)),
                dma((chunks, chips - 1)), dma((chunks, chips - 1)), dma((chunks, chips * CORES - 1)), dma((chunks, chips * CORES - 1))],
            compiler_params=pltpu.CompilerParams(collective_id=0, has_side_effects=True, vmem_limit_bytes=29 << 20),
            name='step',
        )(in_hbm(x), in_hbm(wq), in_hbm(wk), in_hbm(wv), in_hbm(wo), in_hbm(k3), in_hbm(v3), pos, pos2)
        ko, vo = pl.pallas_call(
            patch_kernel,
            out_shape=(pltpu.VMEM(shape4, BF16), pltpu.VMEM(shape4, BF16)),
            in_specs=[vm, vm, vm, sm],
            out_specs=[vm, vm],
            scratch_shapes=[pltpu.VMEM((4, batch * 4, 128), F32), pltpu.VMEM((2, batch * 8, 128), F32)],
            input_output_aliases={0: 0, 1: 1},
            compiler_params=pltpu.CompilerParams(vmem_limit_bytes=8 << 20),
            name='patch',
        )(in_vmem(ko.reshape(shape4)), in_vmem(vo.reshape(shape4)), new, pos)
        return y, ko, vo

    return jax.shard_map(local_step, mesh=mesh, in_specs=in_specs, out_specs=out_specs, check_vma=False)
```

time: 227 us -> 72.3 us (0.32)
  blocking collectives: 106 us -> 0 us
  Pallas kernels: 0 us -> 55.9 us
  matrix products: 46 us -> 0 us
  waiting for transfers between devices: 28.6 us -> 0 us
  other arithmetic: 21.6 us -> 0 us
  between operations: 14.2 us -> 0.67 us
  local copies, waits for them, and re-layouts: 8.72 us -> 15.6 us
    psum x2 -> x0, blocking collectives: 79.5 us -> none  [the longest x1 52.4 us: local_step(): result = lax.psum(part_out, 'seq').astype(jnp.bfloat16)]
    pallas_call x0 -> x2, Pallas kernels: none -> 55.9 us  [the longest x1 54.3 us: local_step(): pl.pallas_call(functools.partial(step_kernel, chips), out_shape=(jax.Shap...]
    dot_general x6 -> x0, matrix products: 46 us -> none  [the longest x1 13.6 us: local_step(): jnp.dot(hidden, w_query, preferred_element_type=jnp.float32)]
    psum x1 -> x0, waiting for transfers between devices: 28.6 us -> none  [local_step(): lax.psum((local_sum * rescale, local_out * rescale[..., None]), 'seq')]
    pmax x1 -> x0, blocking collectives: 26.9 us -> none  [local_step(): global_max = lax.pmax(local_max, 'seq')]
    select_n x2 -> x0, other arithmetic: 17.4 us -> none  [the longest x1 17.4 us: local_step(): k_updated = jnp.where(at_pos, key_new[:, None], k_cache)]
    unnamed x14 -> x9, local copies, waits for them, and re-layouts: 7.17 us -> 14.1 us
    reduce_sum x1 -> x0, other arithmetic: 2.37 us -> none  [local_step(): local_sum = jnp.sum(weights, axis=-1)]
  transfers between devices with their start and end apart: 1 -> 0, of which waited for: 1 -> 0; matrix products, arithmetic and copies ran while one was open for 0% -> 0% of each run, Pallas kernels for 0% -> 0%
where the time goes in v1:
time: 72.3 us; the launch traced here: 72.1 us
  Pallas kernels  55.9 us (77%)
  local copies, waits for them, and re-layouts  15.6 us (22%)
    pallas_call x1, Pallas kernels, local_step(): pl.pallas_call(functools.partial(step_kernel, chips), out_shape=(jax.Shap...  54.3 us
    unnamed x9, local copies, waits for them, and re-layouts  14.1 us
    pallas_call x1, Pallas kernels, local_step(): pl.pallas_call(patch_kernel, out_shape=(pltpu.VMEM(shape4, BF16), pltpu.V...  1.61 us
    broadcast_in_dim x3, local copies, waits for them, and re-layouts, local_step(): pos2 = jnp.repeat(pos, 2).reshape(2, batch)  1.49 us

profile of v1, /device:TPU:113, one launch (start us, length us, event | category | flops | bytes accessed | tf_op | source)
XLA Modules:
  0.0 72.1 jit_solution(4962457707041476936)
XLA Ops:
  0.6 0.7 %broadcast_in_dim.7 = s32[2,32]{1,0:T(2,128)S(1)} reshape(s32[64]{0:T(128)} %pos_ref.3) | data formatting | bytes 512 | tf_op jit(solution)/shard_map/broadcast_in_dim | solution.py:336
  1.4 0.1 broadcast_in_dim.8
  1.4 0.7 broadcast_in_dim.9.pos2_ref
  2.1 0.0 copy-start.1
  2.1 54.3 %step.1 = (bf16[64,4096]{1,0:T(8,128)(2,1)}, bf16[64,1024,128]{2,1,0:T(8,128)(2,1)S(1)}, bf16[64,1024,128]{2,1,0:T(8,128)(2,1)S(1)}, bf16[4,256,128]{2,1,0:T(8,128)(2,1)}) custom-call(bf16[64,4096]{1,0:T(8,128)(2,1)} %x_hbm.1, bf16[4096,4096]{1,0:T(8,128)(2,1)} %wq_hbm.1, bf16[4096,1024]{1,0:T(8,128)(2,1)} %wk_hbm.1, bf16[4096,1024]{1,0:T(8,128)(2,1)} %wv_hbm.1, ...), custom_call_target="tpu_custom_call" | custom-call | tf_op jit(solution)/shard_map/step/pallas_call | solution.py:337
  56.4 0.0 copy-done.1
  56.4 0.0 copy-start
  56.5 0.9 %copy-done = bf16[4,256,128]{2,1,0:T(8,128)(2,1)S(1)} copy-done((bf16[4,256,128]{2,1,0:T(8,128)(2,1)S(1)}, bf16[4,256,128]{2,1,0:T(8,128)(2,1)}, u32[]{:S(2)}) %copy-start) | copy-done | bytes 262168
  57.4 1.6 %patch.1 = (bf16[64,128,8,128]{3,2,1,0:T(8,128)(2,1)S(1)}, bf16[64,128,8,128]{3,2,1,0:T(8,128)(2,1)S(1)}) custom-call(bf16[64,128,8,128]{3,2,1,0:T(8,128)(2,1)S(1)} %bitcast.4, bf16[64,128,8,128]{3,2,1,0:T(8,128)(2,1)S(1)} %bitcast.5, bf16[4,256,128]{2,1,0:T(8,128)(2,1)S(1)} %copy-done, s32[64]{0:T(128)S(1)} %copy-done.1), custom_call_target="tpu_custom_call", output_to_operand_aliasing={{0}: (0, {}), {1}: (1, {})} | custom-call | tf_op jit(solution)/shard_map/patch/pallas_call | solution.py:357
  59.0 6.2 %copy.18 = bf16[64,128,8,128]{3,2,1,0:T(8,128)(2,1)} copy(bf16[64,128,8,128]{3,2,1,0:T(8,128)(2,1)S(1)} %get-tuple-element.16) | data formatting | bytes 33554432
  65.2 0.0 copy-start.2
  65.2 6.2 %copy.19 = bf16[64,128,8,128]{3,2,1,0:T(8,128)(2,1)} copy(bf16[64,128,8,128]{3,2,1,0:T(8,128)(2,1)S(1)} %get-tuple-element.17) | data formatting | bytes 33554432
  71.3 0.0 copy-done.2
  71.3 0.8 %copy.20 = bf16[64,4096]{1,0:T(8,128)(2,1)} copy(bf16[64,4096]{1,0:T(8,128)(2,1)S(1)} %copy-done.2) | data formatting | bytes 1048576
Async XLA Ops:
  2.1 54.3 %copy-start.1 = (s32[64]{0:T(128)S(1)}, s32[64]{0:T(128)}, u32[]{:S(2)}) copy-start(s32[64]{0:T(128)} %pos_ref.3) | copy-start | bytes 772
  56.4 1.0 %copy-start = (bf16[4,256,128]{2,1,0:T(8,128)(2,1)S(1)}, bf16[4,256,128]{2,1,0:T(8,128)(2,1)}, u32[]{:S(2)}) copy-start(bf16[4,256,128]{2,1,0:T(8,128)(2,1)} %get-tuple-element.12.new_ref) | copy-start | bytes 786436
  65.2 6.2 %copy-start.2 = (bf16[64,4096]{1,0:T(8,128)(2,1)S(1)}, bf16[64,4096]{1,0:T(8,128)(2,1)}, u32[]{:S(2)}) copy-start(bf16[64,4096]{1,0:T(8,128)(2,1)} %get-tuple-element.21) | copy-start | bytes 1572868

commit v2 on v1

--- a/solution.py
+++ b/solution.py
@@ -15,10 +15,10 @@
 NT = (((1,), (1,)), ((), ()))
 
 
-def step_kernel(chips, x_hbm, wq_hbm, wk_hbm, wv_hbm, wo_hbm, k_hbm, v_hbm, pos_ref, pos2_ref,
-                y_ref, kout, vout, kv_all,
-                x_v, wbuf, wo_v, qs, q_all, colmask, oraw, mraw, lraw, om, op, orecv, ofin,
-                ys, yp, yr, yfull,
+def step_kernel(chips, x_hbm, wq_hbm, wk_hbm, wv_hbm, wo_hbm, k_hbm, v_hbm, pos_ref,
+                yfull, kout, vout, kv_all,
+                x_v, wbuf, wo_v, qs, q_all, colmask, pos2_ref, oraw, mraw, lraw, om, op, orecv,
+                ys, yp, yr,
                 lsem, kvsem, q_ss, q_rs, n_ss, n_rs, od_s, od_r, oi_s, oi_r, yd_s, yd_r, yi_s, yi_r, ag_s, ag_r):
     batch = k_hbm.shape[0]
     local_len = k_hbm.shape[1] // 8
@@ -36,6 +36,9 @@
         return (rep, lax.rem(c, chips) * CORES + e)
 
     partner = dev(chip, 1 - core)
+    via = lax.rem(chip + 1 + core * (chips - 2), chips)
+    opp = lax.rem(chip + chips - 1 - core * (chips - 2), chips)
+    far = lax.rem(chip + 2, chips)
 
     ncols = 256
     lx = pltpu.make_async_copy(x_hbm, x_v, lsem.at[0])
@@ -59,6 +62,12 @@
     row = lax.broadcasted_iota(jnp.int32, colmask.shape, 0)
     col = lax.broadcasted_iota(jnp.int32, colmask.shape, 1)
     colmask[...] = jnp.where(col % 8 == (row // 16) * 2 + (row % 8) // 4, col, 1 << 30)
+
+    lane_b = (lax.broadcasted_iota(jnp.int32, pos2_ref.shape, 1) + lax.broadcasted_iota(jnp.int32, pos2_ref.shape, 0) * pos2_ref.shape[1]) // 2
+    pv = jnp.zeros(pos2_ref.shape, jnp.int32)
+    for b in range(batch):
+        pv = jnp.where(lane_b == b, pos_ref[b], pv)
+    pos2_ref[...] = pv
 
     lx.wait()
     lk.start()
@@ -199,26 +208,34 @@
     def chip_reduce(i):
         od[i].wait_recv()
         for t in range(4):
-            a, b = om[i, core, t], op[i, t]
-            m, l, (wa, wb) = merge([a, b])
-            for g in range(nrow // 8):
-                r = slice(g * 8, g * 8 + 8)
-                om[i, core, t, g * 8:g * 8 + 8, :] = a[r] * wa[:, g:g + 1] + b[r] * wb[:, g:g + 1]
-            om[i, core, t, nrow:nrow + 8, :] = m
-            om[i, core, t, nrow + 8:nrow + 16, :] = l
-        oi[i] = []
-        for d in range(1, chips):
-            c = pltpu.make_async_remote_copy(om.at[i, core, lax.rem(chip + d, chips)], orecv.at[i, d - 1], oi_s.at[i, d - 1], oi_r.at[i, d - 1],
-                                             device_id=dev(chip + d, core), device_id_type=MESH)
-            c.start()
-            oi[i].append(c)
+            fold(om.at[i, core, t], om[i, core, t], op[i, t])
+        relay = pltpu.make_async_remote_copy(om.at[i, core, far], orecv.at[i, 0], oi_s.at[i, 0], oi_r.at[i, 0], device_id=dev(via, core), device_id_type=MESH)
+        direct = pltpu.make_async_remote_copy(om.at[i, core, opp], orecv.at[i, 1], oi_s.at[i, 1], oi_r.at[i, 1], device_id=dev(opp, core), device_id_type=MESH)
+        relay.start()
+        direct.start()
+        oi[i] = [relay, direct]
+
+    def fold(dst, a, b):
+        m, l, (wa, wb) = merge([a, b])
+        for g in range(nrow // 8):
+            r = slice(g * 8, g * 8 + 8)
+            dst[g * 8:g * 8 + 8, :] = a[r] * wa[:, g:g + 1] + b[r] * wb[:, g:g + 1]
+        dst[nrow:nrow + 8, :] = m
+        dst[nrow + 8:nrow + 16, :] = l
+
+    def o_relay(i):
+        oi[i][0].wait_recv()
+        fold(om.at[i, core, via], om[i, core, via], orecv[i, 0])
+        c = pltpu.make_async_remote_copy(om.at[i, core, via], orecv.at[i, 2], oi_s.at[i, 2], oi_r.at[i, 2], device_id=dev(via, core), device_id_type=MESH)
+        c.start()
+        oi[i].append(c)
 
     def project(i):
-        for c in oi[i]:
+        for c in oi[i][1:]:
             c.wait_recv()
         if i == 0:
             lo.wait()
-        parts = [om[i, core, chip]] + [orecv[i, d] for d in range(chips - 1)]
+        parts = [om[i, core, chip], orecv[i, 1], orecv[i, 2]]
         m, l, ws = merge(parts)
         rl = 1.0 / l
         heads = []
@@ -239,33 +256,50 @@
     def y_chip(i):
         yd[i].wait_recv()
         ys[i, core] = ys[i, core] + yp[i]
-        yi[i] = []
-        for d in range(1, chips):
-            c = pltpu.make_async_remote_copy(ys.at[i, core, lax.rem(chip + d, chips)], yr.at[i, d - 1], yi_s.at[i, d - 1], yi_r.at[i, d - 1],
-                                             device_id=dev(chip + d, core), device_id_type=MESH)
-            c.start()
-            yi[i].append(c)
+        relay = pltpu.make_async_remote_copy(ys.at[i, core, far], yr.at[i, 0], yi_s.at[i, 0], yi_r.at[i, 0], device_id=dev(via, core), device_id_type=MESH)
+        direct = pltpu.make_async_remote_copy(ys.at[i, core, opp], yr.at[i, 1], yi_s.at[i, 1], yi_r.at[i, 1], device_id=dev(opp, core), device_id_type=MESH)
+        relay.start()
+        direct.start()
+        yi[i] = [relay, direct]
+
+    def y_relay(i):
+        yi[i][0].wait_recv()
+        ys[i, core, via] = ys[i, core, via] + yr[i, 0]
+        c = pltpu.make_async_remote_copy(ys.at[i, core, via], yr.at[i, 2], yi_s.at[i, 2], yi_r.at[i, 2], device_id=dev(via, core), device_id_type=MESH)
+        c.start()
+        yi[i].append(c)
+
+    def block(i, c):
+        return (pl.ds(i * cb, cb), pl.ds(pl.multiple_of((core * 4 + c) * 512, 512), 512))
+
+    def push(i, c, slot, target):
+        cp = pltpu.make_async_remote_copy(yfull.at[block(i, c)], yfull.at[block(i, c)], ag_s.at[i, slot], ag_r.at[i, slot],
+                                          device_id=target, device_id_type=MESH)
+        cp.start()
+        ag[i].append(cp)
 
     def y_final(i):
-        for c in yi[i]:
+        for c in yi[i][1:]:
             c.wait_recv()
-        y = ys[i, core, chip]
-        for d in range(chips - 1):
-            y = y + yr[i, d]
-        own = (pl.ds(i * cb, cb), pl.ds(pl.multiple_of((core * 4 + chip) * 512, 512), 512))
-        yfull[own] = y.astype(BF16)
+        yfull[block(i, chip)] = (ys[i, core, chip] + yr[i, 1] + yr[i, 2]).astype(BF16)
         ag[i] = []
-        for d in range(chips):
-            for f in range(CORES):
-                if d or f:
-                    slot = d * CORES + f - 1
-                    c = pltpu.make_async_remote_copy(yfull.at[own], yfull.at[own], ag_s.at[i, slot], ag_r.at[i, slot],
-                                                     device_id=dev(chip + d, lax.rem(core + f, CORES)), device_id_type=MESH)
-                    c.start()
-                    ag[i].append(c)
-
-    stages = ((finalize, 1), (chip_reduce, 2), (project, 4), (y_chip, 5), (y_final, 7))
-    for k in range(2 * chunks + 6):
+        push(i, chip, 0, dev(via, core))
+        push(i, chip, 1, dev(opp, core))
+        push(i, chip, 2, partner)
+
+    def ag_relay(i):
+        ag[i][0].wait_recv()
+        push(i, opp, 3, dev(via, core))
+        push(i, opp, 4, partner)
+        ag[i][1].wait_recv()
+        push(i, via, 5, partner)
+
+    def ag_last(i):
+        ag[i][3].wait_recv()
+        push(i, far, 6, partner)
+
+    stages = ((finalize, 1), (chip_reduce, 2), (o_relay, 4), (project, 6), (y_chip, 7), (y_relay, 9), (y_final, 11), (ag_relay, 13), (ag_last, 15))
+    for k in range(2 * chunks + 14):
         if k < 2 * chunks:
             if k % 2 == 0:
                 lkc[k // 2].wait()
@@ -279,9 +313,8 @@
             if (k - lag) % 2 == 0 and 0 <= i < chunks:
                 stage(i)
     for i in range(chunks):
-        for c in ag[i]:
-            c.wait_recv()
-    y_ref[...] = yfull[...]
+        for slot in (2, 4, 5, 6):
+            ag[i][slot].wait_recv()
     for c in q_copies + n_copies:
         c.wait_send()
     for i in range(chunks):
@@ -289,29 +322,33 @@
             c.wait_send()
 
 
-def patch_kernel(k_in, v_in, new_ref, pos_ref, k_ref, v_ref, src, dst):
-    batch = k_ref.shape[0]
-    local_len = k_ref.shape[1]
+def write_kernel(which, k_in, new_ref, pos_ref, k_out, k_ref, src, dst, bsem):
+    batch, local_len = k_ref.shape[0], k_ref.shape[1] // 8
     base = lax.axis_index('seq') * local_len
     hb = batch // 2
+    pieces = bsem.shape[0]
+    pb = batch // pieces
     for t in range(4):
-        src[t] = new_ref[t].astype(F32)
-    for w in range(2):
-        for t in range(4):
-            for hf in range(2):
-                for k in range(2):
-                    dst[w, pl.ds(hf * hb * 8 + t * 2 + k, hb, stride=8), :] = src[t, pl.ds(hf * 128 + w * 64 + k, hb, stride=2), :]
-
-    def body(b, carry):
-        rel = pos_ref[b] - base
-
-        @pl.when((rel >= 0) & (rel < local_len))
-        def _():
-            r = pl.ds(pl.multiple_of(b * 8, 8), 8)
-            k_ref[b, rel] = dst[0, r, :].astype(BF16)
-            v_ref[b, rel] = dst[1, r, :].astype(BF16)
-        return carry
-    lax.fori_loop(0, batch, body, 0)
+        for hf in range(2):
+            src[t, hf * hb * 2:(hf + 1) * hb * 2, :] = new_ref[t, hf * 128 + which * 64:hf * 128 + which * 64 + 64, :].astype(F32)
+    for t in range(4):
+        for k in range(2):
+            dst[pl.ds(t * 2 + k, batch, stride=8), :] = src[t, pl.ds(k, batch, stride=2), :]
+    bulk = []
+    for i in range(pieces):
+        @pl.loop(i * pb, (i + 1) * pb)
+        def _(b):
+            rel = pos_ref[b] - base
+
+            @pl.when((rel >= 0) & (rel < local_len))
+            def _():
+                k_ref[b, pl.ds(pl.multiple_of(rel * 8, 8), 8), :] = dst[pl.ds(pl.multiple_of(b * 8, 8), 8), :].astype(BF16)
+        part = pl.ds(i * pb, pb)
+        c = pltpu.make_async_copy(k_ref.at[part], k_out.at[part], bsem.at[i])
+        c.start()
+        bulk.append(c)
+    for c in bulk:
+        c.wait()
 
 
 def solution(mesh):
@@ -319,6 +356,7 @@
     in_specs = (P('rep', None), P(), P(), P(), P('seq', None), cache_spec, cache_spec, P('rep'))
     out_specs = (P('rep', None), cache_spec, cache_spec)
     chips = mesh.shape['seq'] // CORES
+    assert chips == 4
     vm = pl.BlockSpec(memory_space=pltpu.VMEM)
     hbm = pl.BlockSpec(memory_space=pl.ANY)
     sm = pl.BlockSpec(memory_space=pltpu.SMEM)
@@ -333,37 +371,39 @@
         dma = pltpu.SemaphoreType.DMA
         in_hbm = lambda a: pltpu.with_memory_space_constraint(a, pltpu.HBM)
         in_vmem = lambda a: pltpu.with_memory_space_constraint(a, pltpu.VMEM)
-        pos2 = jnp.repeat(pos, 2).reshape(2, batch)
         y, ko, vo, new = pl.pallas_call(
             functools.partial(step_kernel, chips),
-            out_shape=(jax.ShapeDtypeStruct((batch, wo.shape[1]), BF16), pltpu.VMEM(k3.shape, BF16), pltpu.VMEM(k3.shape, BF16),
-                       jax.ShapeDtypeStruct((4, batch * 4, 128), BF16)),
-            in_specs=[hbm] * 7 + [sm, vm],
+            out_shape=(pltpu.VMEM((batch, wo.shape[1]), BF16), pltpu.VMEM(k3.shape, BF16), pltpu.VMEM(k3.shape, BF16),
+                       pltpu.VMEM((4, batch * 4, 128), BF16)),
+            in_specs=[hbm] * 7 + [sm],
             out_specs=[vm] * 4,
             scratch_shapes=[
                 pltpu.VMEM((batch, width), BF16), pltpu.VMEM((3, width, 512), BF16), pltpu.VMEM(wo.shape, BF16),
-                pltpu.VMEM((batch * 8, 128), F32), pltpu.VMEM((4, batch * 8, 128), BF16), pltpu.VMEM((64, k3.shape[1]), jnp.int32),
+                pltpu.VMEM((batch * 8, 128), F32), pltpu.VMEM((4, batch * 8, 128), BF16), pltpu.VMEM((64, k3.shape[1]), jnp.int32), pltpu.VMEM((2, batch), jnp.int32),
                 pltpu.VMEM((4, cb * 8, 128), F32), pltpu.VMEM((4, cb * 8, 128), F32), pltpu.VMEM((4, cb * 8, 128), F32),
                 pltpu.VMEM((chunks, CORES, 4, cb * 4 + 16, 128), F32), pltpu.VMEM((chunks, 4, cb * 4 + 16, 128), F32),
-                pltpu.VMEM((chunks, chips - 1, cb * 4 + 16, 128), F32), pltpu.VMEM((cb * 4, 128), F32),
+                pltpu.VMEM((chunks, chips - 1, cb * 4 + 16, 128), F32),
                 pltpu.VMEM((chunks, CORES, 4, cb, 512), F32), pltpu.VMEM((chunks, 4, cb, 512), F32), pltpu.VMEM((chunks, chips - 1, cb, 512), F32),
-                pltpu.VMEM((batch, wo.shape[1]), BF16),
                 dma((6,)), dma((2, chunks)), dma((5,)), dma((5,)), dma((5,)), dma((5,)), dma((chunks,)), dma((chunks,)),
                 dma((chunks, chips - 1)), dma((chunks, chips - 1)), dma((chunks,)), dma((chunks,)),
                 dma((chunks, chips - 1)), dma((chunks, chips - 1)), dma((chunks, chips * CORES - 1)), dma((chunks, chips * CORES - 1))],
             compiler_params=pltpu.CompilerParams(collective_id=0, has_side_effects=True, vmem_limit_bytes=29 << 20),
             name='step',
-        )(in_hbm(x), in_hbm(wq), in_hbm(wk), in_hbm(wv), in_hbm(wo), in_hbm(k3), in_hbm(v3), pos, pos2)
-        ko, vo = pl.pallas_call(
-            patch_kernel,
-            out_shape=(pltpu.VMEM(shape4, BF16), pltpu.VMEM(shape4, BF16)),
-            in_specs=[vm, vm, vm, sm],
-            out_specs=[vm, vm],
-            scratch_shapes=[pltpu.VMEM((4, batch * 4, 128), F32), pltpu.VMEM((2, batch * 8, 128), F32)],
-            input_output_aliases={0: 0, 1: 1},
-            compiler_params=pltpu.CompilerParams(vmem_limit_bytes=8 << 20),
-            name='patch',
-        )(in_vmem(ko.reshape(shape4)), in_vmem(vo.reshape(shape4)), new, pos)
+        )(in_hbm(x), in_hbm(wq), in_hbm(wk), in_hbm(wv), in_hbm(wo), in_hbm(k3), in_hbm(v3), pos)
+        pieces = 8
+
+        def write(which, cache, last):
+            return pl.pallas_call(
+                functools.partial(write_kernel, which),
+                out_shape=(jax.ShapeDtypeStruct(k3.shape, BF16), pltpu.VMEM(k3.shape, BF16)),
+                in_specs=[vm, vm, sm],
+                out_specs=[hbm, vm],
+                scratch_shapes=[pltpu.VMEM((4, batch * 2, 128), F32), pltpu.VMEM((batch * 8, 128), F32), dma((pieces,))],
+                input_output_aliases={0: 1},
+                compiler_params=pltpu.CompilerParams(vmem_limit_bytes=8 << 20),
+                name='write',
+            )(in_vmem(cache), in_vmem(new), pos)[0].reshape(shape4)
+        ko, vo = write(0, ko, False), write(1, vo, True)
         return y, ko, vo
 
     return jax.shard_map(local_step, mesh=mesh, in_specs=in_specs, out_specs=out_specs, check_vma=False)

time: 72.3 us -> 71.8 us (level)
  local copies, waits for them, and re-layouts: 15.6 us -> 0.8 us
  Pallas kernels: 55.9 us -> 70.2 us
    pallas_call x2 -> x3, Pallas kernels: 55.9 us -> 70.2 us  [the longest x1 56.9 us: local_step(): pl.pallas_call(functools.partial(step_kernel, chips), out_shape=(pltpu.VM...]
    unnamed x9 -> x3, local copies, waits for them, and re-layouts: 14.1 us -> 0.8 us
    broadcast_in_dim x3 -> x0, local copies, waits for them, and re-layouts: 1.49 us -> none  [local_step(): pos2 = jnp.repeat(pos, 2).reshape(2, batch)]
where the time goes in v2:
time: 71.8 us; the launch traced here: 71.7 us
  Pallas kernels  70.2 us (98%)
  local copies, waits for them, and re-layouts  0.8 us (1%)
    pallas_call x1, Pallas kernels, local_step(): pl.pallas_call(functools.partial(step_kernel, chips), out_shape=(pltpu.VM...  56.9 us
    pallas_call x2, Pallas kernels, write(): pl.pallas_call(functools.partial(write_kernel, which), out_shape=(jax.Sha...  13.3 us

profile of v2, /device:TPU:113, one launch (start us, length us, event | category | flops | bytes accessed | tf_op | source)
XLA Modules:
  0.0 71.7 jit_solution(17505564215575796076)
XLA Ops:
  0.6 0.0 copy-start
  0.6 56.9 %step.1 = (bf16[64,4096]{1,0:T(8,128)(2,1)S(1)}, bf16[64,1024,128]{2,1,0:T(8,128)(2,1)S(1)}, bf16[64,1024,128]{2,1,0:T(8,128)(2,1)S(1)}, bf16[4,256,128]{2,1,0:T(8,128)(2,1)S(1)}) custom-call(bf16[64,4096]{1,0:T(8,128)(2,1)} %x_hbm.1, bf16[4096,4096]{1,0:T(8,128)(2,1)} %wq_hbm.1, bf16[4096,1024]{1,0:T(8,128)(2,1)} %wk_hbm.1, bf16[4096,1024]{1,0:T(8,128)(2,1)} %wv_hbm.1, ...), custom_call_target="tpu_custom_call" | custom-call | tf_op jit(solution)/shard_map/step/pallas_call | solution.py:374
  57.6 0.8 %copy.16 = bf16[64,4096]{1,0:T(8,128)(2,1)} copy(bf16[64,4096]{1,0:T(8,128)(2,1)S(1)} %get-tuple-element.15) | data formatting | bytes 1048576
  58.4 0.0 copy-done
  58.4 6.7 %write.2 = (bf16[64,1024,128]{2,1,0:T(8,128)(2,1)}, bf16[64,1024,128]{2,1,0:T(8,128)(2,1)S(1)}) custom-call(bf16[64,1024,128]{2,1,0:T(8,128)(2,1)S(1)} %get-tuple-element.10.k_in, bf16[4,256,128]{2,1,0:T(8,128)(2,1)S(1)} %get-tuple-element.11.new_ref, s32[64]{0:T(128)S(1)} %copy-done), custom_call_target="tpu_custom_call", output_to_operand_aliasing={{1}: (0, {})} | custom-call | tf_op jit(solution)/shard_map/write/pallas_call | solution.py:396
  65.0 6.7 %write.3 = (bf16[64,1024,128]{2,1,0:T(8,128)(2,1)}, bf16[64,1024,128]{2,1,0:T(8,128)(2,1)S(1)}) custom-call(bf16[64,1024,128]{2,1,0:T(8,128)(2,1)S(1)} %get-tuple-element.13.k_in, bf16[4,256,128]{2,1,0:T(8,128)(2,1)S(1)} %get-tuple-element.11.new_ref, s32[64]{0:T(128)S(1)} %copy-done), custom_call_target="tpu_custom_call", output_to_operand_aliasing={{1}: (0, {})} | custom-call | tf_op jit(solution)/shard_map/write/pallas_call | solution.py:396
Async XLA Ops:
  0.6 57.7 %copy-start = (s32[64]{0:T(128)S(1)}, s32[64]{0:T(128)}, u32[]{:S(2)}) copy-start(s32[64]{0:T(128)} %pos_ref.5) | copy-start | bytes 772

commit v3 on v2

--- a/solution.py
+++ b/solution.py
@@ -23,6 +23,7 @@
     batch = k_hbm.shape[0]
     local_len = k_hbm.shape[1] // 8
     chunks = om.shape[0]
+    straight = range(1, chunks)
     cb = batch // chunks
     half = batch // 2
     scale2 = k_hbm.shape[2] ** -0.5 * math.log2(math.e)
@@ -87,12 +88,23 @@
         copies = [pltpu.make_async_remote_copy(buf.at[quarter], buf.at[quarter], ss.at[0], rs.at[0], device_id=partner, device_id_type=MESH)]
         for side, shift in ((0, 1), (1, chips - 1)):
             part = pl.ds(side * rows // 2, rows // 2)
-            for f in range(CORES):
-                e = lax.rem(core + f, CORES)
-                slot = 1 + side * 2 + f
-                copies.append(pltpu.make_async_remote_copy(
-                    buf.at[quarter, part], buf.at[quarter, part], ss.at[slot], rs.at[slot], device_id=dev(chip + shift, e), device_id_type=MESH))
+            copies.append(pltpu.make_async_remote_copy(
+                buf.at[quarter, part], buf.at[quarter, part], ss.at[1 + side], rs.at[1 + side], device_id=dev(chip + shift, core), device_id_type=MESH))
         return copies
+
+    def hand_on(copies, buf, rows, ss, rs):
+        other = ((chip + 1) % 2) * CORES + core
+        for side in range(2):
+            copies[1 + side].wait_recv()
+            part = pl.ds(side * rows // 2, rows // 2)
+            c = pltpu.make_async_remote_copy(buf.at[other, part], buf.at[other, part], ss.at[3 + side], rs.at[3 + side], device_id=partner, device_id_type=MESH)
+            c.start()
+            copies.append(c)
+
+    def arrive(copies):
+        copies[0].wait_recv()
+        copies[3].wait_recv()
+        copies[4].wait_recv()
 
     q_copies = spread(q_all, batch * 8, q_ss, q_rs)
     for c in q_copies:
@@ -120,8 +132,9 @@
     bm0 = jnp.where(rowb == 0, 1.0, 0.0).astype(BF16)
     bm1 = jnp.where(rowb == 1, 1.0, 0.0).astype(BF16)
 
-    for c in q_copies:
-        c.wait_recv()
+    hand_on(q_copies, q_all, batch * 8, q_ss, q_rs)
+    hand_on(n_copies, kv_all, batch * 4, n_ss, n_rs)
+    arrive(q_copies)
 
     def pair(pi, loc):
         q = jnp.concatenate([q_all[t, pl.ds(pl.multiple_of(pi * 16, 16), 16), :] for t in range(4)], axis=0)
@@ -209,6 +222,14 @@
         od[i].wait_recv()
         for t in range(4):
             fold(om.at[i, core, t], om[i, core, t], op[i, t])
+        if i in straight:
+            oi[i] = [None]
+            for d in range(1, chips):
+                c = pltpu.make_async_remote_copy(om.at[i, core, lax.rem(chip + d, chips)], orecv.at[i, d - 1], oi_s.at[i, d - 1], oi_r.at[i, d - 1],
+                                                 device_id=dev(chip + d, core), device_id_type=MESH)
+                c.start()
+                oi[i].append(c)
+            return
         relay = pltpu.make_async_remote_copy(om.at[i, core, far], orecv.at[i, 0], oi_s.at[i, 0], oi_r.at[i, 0], device_id=dev(via, core), device_id_type=MESH)
         direct = pltpu.make_async_remote_copy(om.at[i, core, opp], orecv.at[i, 1], oi_s.at[i, 1], oi_r.at[i, 1], device_id=dev(opp, core), device_id_type=MESH)
         relay.start()
@@ -235,7 +256,7 @@
             c.wait_recv()
         if i == 0:
             lo.wait()
-        parts = [om[i, core, chip], orecv[i, 1], orecv[i, 2]]
+        parts = [om[i, core, chip]] + [orecv[i, d] for d in range(0 if i in straight else 1, chips - 1)]
         m, l, ws = merge(parts)
         rl = 1.0 / l
         heads = []
@@ -256,6 +277,14 @@
     def y_chip(i):
         yd[i].wait_recv()
         ys[i, core] = ys[i, core] + yp[i]
+        if i in straight:
+            yi[i] = [None]
+            for d in range(1, chips):
+                c = pltpu.make_async_remote_copy(ys.at[i, core, lax.rem(chip + d, chips)], yr.at[i, d - 1], yi_s.at[i, d - 1], yi_r.at[i, d - 1],
+                                                 device_id=dev(chip + d, core), device_id_type=MESH)
+                c.start()
+                yi[i].append(c)
+            return
         relay = pltpu.make_async_remote_copy(ys.at[i, core, far], yr.at[i, 0], yi_s.at[i, 0], yi_r.at[i, 0], device_id=dev(via, core), device_id_type=MESH)
         direct = pltpu.make_async_remote_copy(ys.at[i, core, opp], yr.at[i, 1], yi_s.at[i, 1], yi_r.at[i, 1], device_id=dev(opp, core), device_id_type=MESH)
         relay.start()
@@ -272,57 +301,58 @@
     def block(i, c):
         return (pl.ds(i * cb, cb), pl.ds(pl.multiple_of((core * 4 + c) * 512, 512), 512))
 
-    def push(i, c, slot, target):
-        cp = pltpu.make_async_remote_copy(yfull.at[block(i, c)], yfull.at[block(i, c)], ag_s.at[i, slot], ag_r.at[i, slot],
-                                          device_id=target, device_id_type=MESH)
-        cp.start()
-        ag[i].append(cp)
-
     def y_final(i):
         for c in yi[i][1:]:
             c.wait_recv()
-        yfull[block(i, chip)] = (ys[i, core, chip] + yr[i, 1] + yr[i, 2]).astype(BF16)
+        y = ys[i, core, chip]
+        for d in range(0 if i in straight else 1, chips - 1):
+            y = y + yr[i, d]
+        own = block(i, chip)
+        yfull[own] = y.astype(BF16)
         ag[i] = []
-        push(i, chip, 0, dev(via, core))
-        push(i, chip, 1, dev(opp, core))
-        push(i, chip, 2, partner)
-
-    def ag_relay(i):
-        ag[i][0].wait_recv()
-        push(i, opp, 3, dev(via, core))
-        push(i, opp, 4, partner)
-        ag[i][1].wait_recv()
-        push(i, via, 5, partner)
-
-    def ag_last(i):
-        ag[i][3].wait_recv()
-        push(i, far, 6, partner)
-
-    stages = ((finalize, 1), (chip_reduce, 2), (o_relay, 4), (project, 6), (y_chip, 7), (y_relay, 9), (y_final, 11), (ag_relay, 13), (ag_last, 15))
-    for k in range(2 * chunks + 14):
+        for d in range(chips):
+            for f in range(CORES):
+                if d or f:
+                    slot = d * CORES + f - 1
+                    c = pltpu.make_async_remote_copy(yfull.at[own], yfull.at[own], ag_s.at[i, slot], ag_r.at[i, slot],
+                                                     device_id=dev(chip + d, lax.rem(core + f, CORES)), device_id_type=MESH)
+                    c.start()
+                    ag[i].append(c)
+
+    relayed = ((finalize, 1), (chip_reduce, 2), (o_relay, 4), (project, 6), (y_chip, 7), (y_relay, 8), (y_final, 9))
+    direct_early = ((finalize, 1), (chip_reduce, 2), (project, 4), (y_chip, 5), (y_final, 7))
+    direct_late = ((finalize, 1), (chip_reduce, 2), (project, 3), (y_chip, 4), (y_final, 5))
+    plan = {}
+    for i in range(chunks):
+        for stage, lag in direct_late if i >= chunks - 2 else direct_early if i in straight else relayed:
+            plan.setdefault(2 * i + lag, []).append((stage, i))
+    for k in range(max(plan) + 1):
         if k < 2 * chunks:
             if k % 2 == 0:
                 lkc[k // 2].wait()
                 lvc[k // 2].wait()
             attend(k // 2, k % 2)
         if k == 1:
-            for c in n_copies:
-                c.wait_recv()
-        for stage, lag in stages:
-            i = (k - lag) // 2
-            if (k - lag) % 2 == 0 and 0 <= i < chunks:
-                stage(i)
+            arrive(n_copies)
+        for stage, i in plan.get(k, ()):
+            stage(i)
     for i in range(chunks):
-        for slot in (2, 4, 5, 6):
-            ag[i][slot].wait_recv()
+        for c in ag[i]:
+            c.wait_recv()
     for c in q_copies + n_copies:
         c.wait_send()
     for i in range(chunks):
         for c in [od[i], yd[i]] + oi[i] + yi[i] + ag[i]:
-            c.wait_send()
-
-
-def write_kernel(which, k_in, new_ref, pos_ref, k_out, k_ref, src, dst, bsem):
+            if c is not None:
+                c.wait_send()
+
+
+def write_kernel(which, k_in, new_ref, pos_ref, *refs):
+    if which == 0:
+        y_ref, k_out, k_ref, y_out, src, dst, bsem, ysem = refs
+        cy = pltpu.make_async_copy(y_ref, y_out, ysem)
+    else:
+        k_out, k_ref, src, dst, bsem, ysem = refs
     batch, local_len = k_ref.shape[0], k_ref.shape[1] // 8
     base = lax.axis_index('seq') * local_len
     hb = batch // 2
@@ -347,6 +377,9 @@
         c = pltpu.make_async_copy(k_ref.at[part], k_out.at[part], bsem.at[i])
         c.start()
         bulk.append(c)
+    if which == 0:
+        cy.start()
+        bulk.append(cy)
     for c in bulk:
         c.wait()
 
@@ -392,18 +425,19 @@
         )(in_hbm(x), in_hbm(wq), in_hbm(wk), in_hbm(wv), in_hbm(wo), in_hbm(k3), in_hbm(v3), pos)
         pieces = 8
 
-        def write(which, cache, last):
+        def write(which, cache, *extra):
             return pl.pallas_call(
                 functools.partial(write_kernel, which),
-                out_shape=(jax.ShapeDtypeStruct(k3.shape, BF16), pltpu.VMEM(k3.shape, BF16)),
-                in_specs=[vm, vm, sm],
-                out_specs=[hbm, vm],
-                scratch_shapes=[pltpu.VMEM((4, batch * 2, 128), F32), pltpu.VMEM((batch * 8, 128), F32), dma((pieces,))],
+                out_shape=(jax.ShapeDtypeStruct(k3.shape, BF16), pltpu.VMEM(k3.shape, BF16), *(jax.ShapeDtypeStruct(e.shape, BF16) for e in extra)),
+                in_specs=[vm, vm, sm] + [vm] * len(extra),
+                out_specs=[hbm, vm] + [hbm] * len(extra),
+                scratch_shapes=[pltpu.VMEM((4, batch * 2, 128), F32), pltpu.VMEM((batch * 8, 128), F32), dma((pieces,)), dma],
                 input_output_aliases={0: 1},
                 compiler_params=pltpu.CompilerParams(vmem_limit_bytes=8 << 20),
                 name='write',
-            )(in_vmem(cache), in_vmem(new), pos)[0].reshape(shape4)
-        ko, vo = write(0, ko, False), write(1, vo, True)
-        return y, ko, vo
+            )(in_vmem(cache), in_vmem(new), pos, *(in_vmem(e) for e in extra))
+        ko, _, y = write(0, ko, y)
+        vo, _ = write(1, vo)
+        return y, ko.reshape(shape4), vo.reshape(shape4)
 
     return jax.shard_map(local_step, mesh=mesh, in_specs=in_specs, out_specs=out_specs, check_vma=False)

time: 71.8 us -> 70.2 us (0.978)
  Pallas kernels: 70.2 us -> 69.4 us
  local copies, waits for them, and re-layouts: 0.8 us -> 0.01 us
    pallas_call x1, Pallas kernels: 56.9 us -> 56 us  [local_step(): pl.pallas_call(functools.partial(step_kernel, chips), out_shape=(pltpu.VM...]
    unnamed x3 -> x2, local copies, waits for them, and re-layouts: 0.8 us -> 0.01 us
where the time goes in v3:
time: 70.2 us; the launch traced here: 70.1 us
  Pallas kernels  69.4 us (99%)
    pallas_call x1, Pallas kernels, local_step(): pl.pallas_call(functools.partial(step_kernel, chips), out_shape=(pltpu.VM...  56 us
    pallas_call x2, Pallas kernels, write(): pl.pallas_call(functools.partial(write_kernel, which), out_shape=(jax.Sha...  13.4 us

profile of v3, /device:TPU:113, one launch (start us, length us, event | category | flops | bytes accessed | tf_op | source)
XLA Modules:
  0.0 70.1 jit_solution(4111204268392152130)
XLA Ops:
  0.6 0.0 copy-start
  0.6 56.0 %step.1 = (bf16[64,4096]{1,0:T(8,128)(2,1)S(1)}, bf16[64,1024,128]{2,1,0:T(8,128)(2,1)S(1)}, bf16[64,1024,128]{2,1,0:T(8,128)(2,1)S(1)}, bf16[4,256,128]{2,1,0:T(8,128)(2,1)S(1)}) custom-call(bf16[64,4096]{1,0:T(8,128)(2,1)} %x_hbm.1, bf16[4096,4096]{1,0:T(8,128)(2,1)} %wq_hbm.1, bf16[4096,1024]{1,0:T(8,128)(2,1)} %wk_hbm.1, bf16[4096,1024]{1,0:T(8,128)(2,1)} %wv_hbm.1, ...), custom_call_target="tpu_custom_call" | custom-call | tf_op jit(solution)/shard_map/step/pallas_call | solution.py:407
  56.6 0.0 copy-done
  56.6 6.8 %write.2 = (bf16[64,1024,128]{2,1,0:T(8,128)(2,1)}, bf16[64,1024,128]{2,1,0:T(8,128)(2,1)S(1)}, bf16[64,4096]{1,0:T(8,128)(2,1)}) custom-call(bf16[64,1024,128]{2,1,0:T(8,128)(2,1)S(1)} %get-tuple-element.10.k_in, bf16[4,256,128]{2,1,0:T(8,128)(2,1)S(1)} %get-tuple-element.11.new_ref, s32[64]{0:T(128)S(1)} %copy-done, ...), custom_call_target="tpu_custom_call", output_to_operand_aliasing={{1}: (0, {})} | custom-call | tf_op jit(solution)/shard_map/write/pallas_call | solution.py:429
  63.4 6.7 %write.3 = (bf16[64,1024,128]{2,1,0:T(8,128)(2,1)}, bf16[64,1024,128]{2,1,0:T(8,128)(2,1)S(1)}) custom-call(bf16[64,1024,128]{2,1,0:T(8,128)(2,1)S(1)} %get-tuple-element.15.k_in, bf16[4,256,128]{2,1,0:T(8,128)(2,1)S(1)} %get-tuple-element.11.new_ref, s32[64]{0:T(128)S(1)} %copy-done), custom_call_target="tpu_custom_call", output_to_operand_aliasing={{1}: (0, {})} | custom-call | tf_op jit(solution)/shard_map/write/pallas_call | solution.py:429
Async XLA Ops:
  0.6 56.0 %copy-start = (s32[64]{0:T(128)S(1)}, s32[64]{0:T(128)}, u32[]{:S(2)}) copy-start(s32[64]{0:T(128)} %pos_ref.5) | copy-start | bytes 772
